TPU v7x, 32 devices: a whole 2x2x4 slice. The times are simulated.
32 devices in a mesh: tile: 16 (over z, y, x), lev: 2 (over core).
Axes of the slice: x: 2, y: 2, z: 4, core: 2. Of those that a mesh axis runs over, the one named last changes fastest.
Arguments:
- increments: bfloat16 [136, 256, 1024], P('lev', 'tile'), may hold values from -30 to 30
- projection: bfloat16 [80, 136], replicated, may hold values from -0.5 to 0.5
- helmholtz: float32 [80], P('lev'), may hold values from 0.05 to 4
Outputs:
- solution: float32 [80, 256, 1024], P('lev', 'tile')
- residual: float32 [80, 256, 1024], P('lev', 'tile')
All inputs are finite; a program needn't handle non-finite values.
Results may differ from a plain program's by a relative error of at most 0.00075.
Values may be sent and summed in bfloat16 or wider, within the bound.
A program may use at most 192 MiB of HBM per device.

v0:
```python
import jax
import jax.numpy as jnp
import numpy as np
from jax import lax
from jax.sharding import PartitionSpec as P

S = 4
BLOCKS = 2


highest = lax.Precision.HIGHEST


def extended(block, sides, width):
    for axis, dim in sides:
        count = lax.axis_size(axis)
        forward = [(i, i + 1) for i in range(count - 1)]
        backward = [(target, source) for source, target in forward]
        low = lax.ppermute(
            lax.slice_in_dim(block, block.shape[dim] - width, None, axis=dim), axis, forward
        )
        high = lax.ppermute(lax.slice_in_dim(block, 0, width, axis=dim), axis, backward)
        block = jnp.concatenate([low, block, high], axis=dim)
    return block


def shift_matrix():
    width = 2 * S + 1
    table = np.zeros((width, width), np.float32)
    for index in range(S):
        table[index + 1, index] = 1.0
    for index in range(S - 1):
        table[S + 2 + index, S + 1 + index] = 1.0
    return jnp.asarray(table, jnp.float32)


def stencil_rows(field, weight_col):
    padded = extended(field, (("tile", 1),), 1)
    side = jnp.pad(field, ((0, 0), (0, 0), (1, 1)))
    beside_all = padded[:, 2:, :] + padded[:, :-2, :] + side[:, :, 2:] + side[:, :, :-2]
    return weight_col * beside_all


def quadratic(gram, left, right):
    return jnp.einsum("ma,mab,mb->m", left, gram, right, precision=highest)


def combine(coef, vectors):
    total = coef[:, 0, None, None] * vectors[0]
    for index in range(1, len(vectors)):
        total = total + coef[:, index, None, None] * vectors[index]
    return total


def inner_table(vectors):
    width = len(vectors)
    cached = {}
    for first in range(width):
        for second in range(first, width):
            cached[first, second] = jnp.sum(vectors[first] * vectors[second], axis=(1, 2))
    rows_list = []
    for first in range(width):
        entries = []
        for second in range(width):
            entries.append(cached[min(first, second), max(first, second)])
        rows_list.append(jnp.stack(entries, axis=1))
    return jnp.stack(rows_list, axis=1)


def shards(increments, projection, helmholtz):
    lev_count, rows_x, cells_y = increments.shape
    mode_count = projection.shape[0] // lax.axis_size("lev")
    flat = increments.reshape(lev_count, rows_x * cells_y)
    own_cols = lax.dynamic_slice_in_dim(projection, lax.axis_index("lev") * lev_count, lev_count, 1)
    modal = lax.psum_scatter(
        jnp.dot(own_cols, flat, preferred_element_type=jnp.float32),
        "lev",
        scatter_dimension=0,
        tiled=True,
    )
    modal = modal.reshape(mode_count, rows_x, cells_y)
    weight_col = (1.0 / (4.0 + helmholtz))[:, None, None]
    width = 2 * S + 1
    shifter = shift_matrix()
    solution = jnp.zeros_like(modal)
    resid = modal
    direction = modal
    for block_index in range(BLOCKS):
        vectors = [direction]
        current = direction
        for power_index in range(S):
            current = stencil_rows(current, weight_col)
            vectors.append(current)
        vectors.append(resid)
        current = resid
        for power_index in range(S - 1):
            current = stencil_rows(current, weight_col)
            vectors.append(current)
        gram = inner_table(vectors)
        gram = lax.psum(gram, "tile")
        p_coef = jnp.zeros((mode_count, width), jnp.float32).at[:, 0].set(1.0)
        r_coef = jnp.zeros((mode_count, width), jnp.float32).at[:, S + 1].set(1.0)
        x_coef = jnp.zeros((mode_count, width), jnp.float32)
        squares = quadratic(gram, r_coef, r_coef)
        for step_index in range(S):
            moved = p_coef - jnp.einsum("ab,mb->ma", shifter, p_coef, precision=highest)
            alpha = (squares / quadratic(gram, p_coef, moved))[:, None]
            x_coef = x_coef + alpha * p_coef
            r_coef = r_coef - alpha * moved
            fresh = quadratic(gram, r_coef, r_coef)
            p_coef = r_coef + (fresh / squares)[:, None] * p_coef
            squares = fresh
        solution = solution + combine(x_coef, vectors)
        resid = combine(r_coef, vectors)
        direction = combine(p_coef, vectors)
    return (solution, resid)


def solution(mesh):
    in_specs = (P("lev", "tile", None), P(), P("lev"))
    out_specs = (P("lev", "tile", None), P("lev", "tile", None))
    return jax.shard_map(shards, mesh=mesh, in_specs=in_specs, out_specs=out_specs, check_vma=False)
```

profile of v0, /device:TPU:0, one launch (start us, length us, event | category | flops | bytes accessed | tf_op | source)
XLA Modules:
  0.0 469.2 jit_solution(7739262353369601456)
XLA Ops:
  7.2 2.0 pad.144
  9.2 2.9 copy.235
  12.1 4.9 %fusion.44 = f32[80,16384]{1,0:T(8,128)} fusion(bf16[68,16384]{1,0:T(8,128)(2,1)} %bitcast.230, bf16[80,136]{0,1:T(8,128)(2,1)S(1)} %copy-done, s32[]{:T(128)S(6)} %select_n.3), kind=kOutput, calls=%fused_computation.212 | convolution fusion | flops 178257920 | bytes 7489540 | tf_op jit(solution)/shard_map/dot_general | solution.py:76
  17.0 15.9 %reduce-scatter.2.cloned.1.call-done = f32[40,16384]{1,0:T(8,128)} async-done(((f32[80,16384]{1,0:T(8,128)}), f32[40,16384]{1,0:T(8,128)}) %reduce-scatter.2.cloned.1.call-update) | async-done | bytes 2621456 | tf_op jit(solution)/shard_map/reduce_scatter | solution.py:75
  32.9 2.0 copy.251
  35.0 1.3 collective-permute-start
  36.3 4.6 collective-permute-start.1
  40.9 2.4 collective-permute-done
  43.3 4.5 collective-permute-done.1
  47.8 1.4 fusion.2
  52.1 5.0 %collective-permute-start.3 = (f32[40,1,1024]{2,0,1:T(8,128)S(1)}, f32[40,1,1024]{2,0,1:T(8,128)S(1)}, u32[]{:S(2)}, u32[]{:S(2)}) collective-permute-start(f32[40,1,1024]{2,0,1:T(8,128)S(1)} %get-tuple-element.129), channel_id=1, source_target_pairs={{0,2},{2,4},{4,6},{6,8},{8,10},{10,12},{12,14},{14,16},{16,18},{18... | collective-permute-start | bytes 491528 | tf_op jit(solution)/shard_map/ppermute | solution.py:19
  59.9 1.9 collective-permute-done.3
  61.8 5.6 %fusion.5 = f32[40,16,1024]{2,0,1:T(8,128)S(1)} fusion(f32[40,16,1024]{2,0,1:T(8,128)} %copy-done.18, f32[40,1,1024]{2,0,1:T(8,128)S(1)} %collective-permute-done.3, f32[40,1,1024]{2,0,1:T(8,128)S(1)} %collective-permute-done.2, f32[40]{0:T(128)S(1)} %add_divide_fusion), kind=kLoop, calls=%fused_computation.27 | loop fusion | flops 3932160 | bytes 5570720 | tf_op jit(solution)/shard_map/mul | solution.py:41
  69.6 5.0 %collective-permute-start.5 = (f32[40,1,1024]{2,0,1:T(8,128)}, f32[40,1,1024]{2,0,1:T(8,128)S(1)}, u32[]{:S(2)}, u32[]{:S(2)}) collective-permute-start(f32[40,1,1024]{2,0,1:T(8,128)} %get-tuple-element.127), channel_id=1, source_target_pairs={{0,2},{2,4},{4,6},{6,8},{8,10},{10,12},{12,14},{14,16},{16,18},{18... | collective-permute-start | bytes 491528 | tf_op jit(solution)/shard_map/ppermute | solution.py:19
  75.0 2.3 collective-permute-done.4
  77.3 4.5 collective-permute-done.5
  81.8 5.5 %fusion.8 = f32[40,16,1024]{2,0,1:T(8,128)S(1)} fusion(f32[40,16,1024]{2,0,1:T(8,128)} %copy-done.6, f32[40,1,1024]{2,0,1:T(8,128)S(1)} %collective-permute-done.5, f32[40,1,1024]{2,0,1:T(8,128)S(1)} %collective-permute-done.4, f32[40]{0:T(128)S(1)} %add_divide_fusion), kind=kLoop, calls=%fused_computation.30 | loop fusion | flops 3932160 | bytes 5570720 | tf_op jit(solution)/shard_map/mul | solution.py:41
  87.4 1.6 collective-permute-start.6
  88.9 4.9 %collective-permute-start.7 = (f32[40,1,1024]{2,0,1:T(8,128)S(1)}, f32[40,1,1024]{2,0,1:T(8,128)S(1)}, u32[]{:S(2)}, u32[]{:S(2)}) collective-permute-start(f32[40,1,1024]{2,0,1:T(8,128)S(1)} %get-tuple-element.125), channel_id=1, source_target_pairs={{0,2},{2,4},{4,6},{6,8},{8,10},{10,12},{12,14},{14,16},{16,18},{18... | collective-permute-start | bytes 491528 | tf_op jit(solution)/shard_map/ppermute | solution.py:19
  94.1 2.2 collective-permute-done.6
  96.3 2.2 collective-permute-done.7
  98.5 5.4 %multiply_reduce_fusion.45 = (f32[40]{0:T(128)S(1)}, f32[40]{0:T(128)S(1)}, f32[40]{0:T(128)S(1)}, f32[40]{0:T(128)S(1)}, f32[40]{0:T(128)S(1)}, /*index=5*/f32[...) fusion(f32[40,16,1024]{2,0,1:T(8,128)S(1)} %fusion.8, ...), kind=kLoop, calls=%fused_computation.138 | loop fusion | flops 26213840 | bytes 11143520 | tf_op jit(solution)/shard_map/reduce_sum | solution.py:60
  104.2 75.3 %psum.14 = f32[40,9,9]{0,2,1:T(8,128)S(1)} all-reduce(f32[40,9,9]{0,2,1:T(8,128)S(1)} %constant_dynamic-update-slice_fusion), channel_id=1, replica_groups=mesh['tile'=16,'lev'=2] {'tile'}, use_global_device_ids=true, to_apply=%region_17.18 | all-reduce | flops 3240 | bytes 25920 | tf_op jit(solution)/shard_map/psum | solution.py:100
  183.8 13.6 %multiply_add_fusion.2 = f32[40,16,1024]{2,0,1:T(8,128)S(1)} fusion(f32[40,16,1024]{2,0,1:T(8,128)} %copy-done.6, f32[40,16,1024]{2,0,1:T(8,128)} %get-tuple-element.109, f32[40]{0:T(128)S(1)} %get-tuple-element.162, f32[40]{0:T(128)S(1)} %get-tuple-element.163, f32[40]{0:T(128)S(1)} %get-tuple-element.164, f32[40]{0:T(128)S(1)} %get-tuple-element.165, ...), kind=kLoop, calls=%fused_computation.137 | loop fusion | flops 19005440 | bytes 13764160 | tf_op jit(solution)/shard_map/add | solution.py:51
  198.7 4.6 collective-permute-start.9
  203.3 5.8 %multiply_add_fusion.1 = f32[40,16,1024]{2,0,1:T(8,128)S(1)} fusion(f32[40,16,1024]{2,0,1:T(8,128)S(1)} %copy-done.7, f32[40,16,1024]{2,0,1:T(8,128)S(1)} %copy-done.17, f32[40]{0:T(128)S(1)} %get-tuple-element.171, f32[40]{0:T(128)S(1)} %get-tuple-element.172, f32[40]{0:T(128)S(1)} %get-tuple-element.173, f32[40]{0:T(128)S(1)} %get-tuple-element.174, ...), kind=kLoop, calls=%fused_computation.131 | loop fusion | flops 19005440 | bytes 13764160 | tf_op jit(solution)/shard_map/add | solution.py:51
  209.2 1.4 fusion.14
  211.9 4.6 collective-permute-start.11
  217.8 4.6 collective-permute-start.17
  222.4 1.4 fusion.17
  225.2 5.0 %collective-permute-start.13 = (f32[40,1,1024]{2,0,1:T(8,128)S(1)}, f32[40,1,1024]{2,0,1:T(8,128)S(1)}, u32[]{:S(2)}, u32[]{:S(2)}) collective-permute-start(f32[40,1,1024]{2,0,1:T(8,128)S(1)} %get-tuple-element.115), channel_id=1, source_target_pairs={{0,2},{2,4},{4,6},{6,8},{8,10},{10,12},{12,14},{14,16},{16,18},{18... | collective-permute-start | bytes 491528 | tf_op jit(solution)/shard_map/ppermute | solution.py:19
  230.2 2.3 collective-permute-done.12
  232.6 2.0 collective-permute-done.13
  234.5 3.3 fusion.20
  239.2 6.9 %collective-permute-start.19 = (f32[40,1,1024]{2,0,1:T(8,128)S(1)}, f32[40,1,1024]{2,0,1:T(8,128)S(1)}, u32[]{:S(2)}, u32[]{:S(2)}) collective-permute-start(f32[40,1,1024]{2,0,1:T(8,128)S(1)} %get-tuple-element.121), channel_id=1, source_target_pairs={{0,2},{2,4},{4,6},{6,8},{8,10},{10,12},{12,14},{14,16},{16,18},{18... | collective-permute-start | bytes 491528 | tf_op jit(solution)/shard_map/ppermute | solution.py:19
  246.1 1.3 collective-permute-start.14
  247.4 6.1 %collective-permute-start.15 = (f32[40,1,1024]{2,0,1:T(8,128)S(1)}, f32[40,1,1024]{2,0,1:T(8,128)}, u32[]{:S(2)}, u32[]{:S(2)}) collective-permute-start(f32[40,1,1024]{2,0,1:T(8,128)S(1)} %get-tuple-element.113), channel_id=1, source_target_pairs={{0,2},{2,4},{4,6},{6,8},{8,10},{10,12},{12,14},{14,16},{16,18},{18... | collective-permute-start | bytes 491528 | tf_op jit(solution)/shard_map/ppermute | solution.py:19
  253.6 1.4 fusion.29
  255.1 1.5 copy-done.20
  257.8 5.7 %collective-permute-start.21 = (f32[40,1,1024]{2,0,1:T(8,128)S(1)}, f32[40,1,1024]{2,0,1:T(8,128)}, u32[]{:S(2)}, u32[]{:S(2)}) collective-permute-start(f32[40,1,1024]{2,0,1:T(8,128)S(1)} %get-tuple-element.111), channel_id=1, source_target_pairs={{0,2},{2,4},{4,6},{6,8},{8,10},{10,12},{12,14},{14,16},{16,18},{18... | collective-permute-start | bytes 491528 | tf_op jit(solution)/shard_map/ppermute | solution.py:19
  264.3 1.4 collective-permute-done.21
  265.7 24.5 %multiply_reduce_fusion = (f32[40]{0:T(128)}, f32[40]{0:T(128)}, f32[40]{0:T(128)}, f32[40]{0:T(128)}, f32[40]{0:T(128)}, /*index=5*/f32[40]{0:T(128)}, f32[40]{...) fusion(f32[40,16,1024]{2,0,1:T(8,128)} %copy-done.20, ...), kind=kLoop, calls=%fused_computation.91 | loop fusion | flops 70777080 | bytes 21961920 | tf_op jit(solution)/shard_map/reduce_sum | solution.py:60
  290.4 1.4 stack.467
  291.8 1.4 stack.464
  293.2 1.4 stack.460
  294.5 1.4 stack.455
  295.9 1.4 stack.449
  297.3 1.4 stack.442
  298.7 1.3 stack.434
  300.1 1.3 stack.425
  301.4 1.4 stack.415
  308.2 77.3 %psum.15 = f32[40,9,9]{0,2,1:T(8,128)S(1)} all-reduce(f32[40,9,9]{0,2,1:T(8,128)} %constant_dynamic-update-slice_fusion.9), channel_id=1, replica_groups=mesh['tile'=16,'lev'=2] {'tile'}, use_global_device_ids=true, to_apply=%region_64.65 | all-reduce | flops 3240 | bytes 25920 | tf_op jit(solution)/shard_map/psum | solution.py:100
  385.5 1.4 multiply_reduce_fusion.66
  386.9 1.4 copy.117
  388.3 1.4 multiply_reduce_fusion.83
  393.7 1.4 copy.126
  399.5 1.4 copy.139
  408.7 1.4 copy.153
  410.1 1.4 copy.157
  414.2 1.4 copy.166
  422.2 19.2 %multiply_add_fusion = f32[40,16,1024]{2,0,1:T(8,128)} fusion(f32[40,16,1024]{2,0,1:T(8,128)} %get-tuple-element.108, f32[40,16,1024]{2,0,1:T(8,128)} %copy-done.15, f32[40,16,1024]{2,0,1:T(8,128)} %copy-done.11, f32[40,16,1024]{2,0,1:T(8,128)} %get-tuple-element.107, f32[40,16,1024]{2,0,1:T(8,128)} %copy-done.16, f32[40,16,1024]{2,0,1:T(8,128)} %copy-done.13, ...), kind=kLoop, calls=%fused_computation.89 | loop fusion | flops 19005440 | bytes 21628480 | tf_op jit(solution)/shard_map/add | solution.py:51
  441.5 4.9 %copy.22 = f32[40,16,1024]{2,1,0:T(8,128)} copy(f32[40,16,1024]{2,0,1:T(8,128)} %multiply_add_fusion) | data formatting | bytes 5242880
  446.5 12.8 %add_add_fusion = f32[40,16,1024]{2,0,1:T(8,128)S(1)} fusion(f32[40,16,1024]{2,0,1:T(8,128)} %get-tuple-element.108, f32[40,16,1024]{2,0,1:T(8,128)} %copy-done.15, f32[40,16,1024]{2,0,1:T(8,128)S(1)} %copy-done.12, f32[40,16,1024]{2,0,1:T(8,128)} %get-tuple-element.107, f32[40,16,1024]{2,0,1:T(8,128)} %copy-done.16, f32[40,16,1024]{2,0,1:T(8,128)S(1)} %copy-done.14, ...), kind=kLoop, calls=%fused_computation.90 | loop fusion | flops 38666240 | bytes 32771040 | tf_op jit(solution)/shard_map/add | solution.py:113
  459.3 3.0 copy.21
  (303 shorter events, 51.3 us)
Async XLA Ops:
  7.2 25.7 %reduce-scatter.2.cloned.1.call-start = ((), (), s32[]{:S(2)}) async-start(), calls=%async_computation.1 | async-start | bytes 7864320 | tf_op jit(solution)/shard_map/reduce_scatter | solution.py:75
  32.9 8.0 %copy-start.72 = (f32[40]{0:T(128)S(1)}, f32[40]{0:T(128)}, u32[]{:S(2)}) copy-start(f32[40]{0:T(128)} %param.14) | copy-start | bytes 484
  34.9 14.3 %copy-start.3 = (f32[5,16,8,1024]{3,2,0,1:T(8,128)}, f32[5,16,8,1024]{3,2,0,1:T(8,128)S(1)}, u32[]{:S(2)}) copy-start(f32[5,16,8,1024]{3,2,0,1:T(8,128)S(1)} %copy.251) | copy-start | bytes 7864324
  35.0 8.3 %collective-permute-start = (f32[40,1,1024]{2,0,1:T(8,128)S(1)}, f32[40,1,1024]{2,0,1:T(8,128)S(1)}, u32[]{:S(2)}, u32[]{:S(2)}) collective-permute-start(f32[40,1,1024]{2,0,1:T(8,128)S(1)} %get-tuple-element.130), channel_id=1, source_target_pairs={{2,0},{4,2},{6,4},{8,6},{10,8},{12,10},{14,12},{16,14},{18,16},{20... | collective-permute-start | bytes 491528 | tf_op jit(solution)/shard_map/ppermute | solution.py:22
  36.3 11.5 %collective-permute-start.1 = (f32[40,1,1024]{2,0,1:T(8,128)S(1)}, f32[40,1,1024]{2,0,1:T(8,128)S(1)}, u32[]{:S(2)}, u32[]{:S(2)}) collective-permute-start(f32[40,1,1024]{2,0,1:T(8,128)S(1)} %get-tuple-element.131), channel_id=1, source_target_pairs={{0,2},{2,4},{4,6},{6,8},{8,10},{10,12},{12,14},{14,16},{16,18},{18... | collective-permute-start | bytes 491528 | tf_op jit(solution)/shard_map/ppermute | solution.py:19
  40.9 142.9 %copy-start.35 = (f32[40]{0:T(128)}, f32[40]{0:T(128)S(1)}, u32[]{:S(2)}) copy-start(f32[40]{0:T(128)S(1)} %add_divide_fusion) | copy-start | bytes 484
  50.8 9.1 %collective-permute-start.2 = (f32[40,1,1024]{2,0,1:T(8,128)}, f32[40,1,1024]{2,0,1:T(8,128)S(1)}, u32[]{:S(2)}, u32[]{:S(2)}) collective-permute-start(f32[40,1,1024]{2,0,1:T(8,128)} %get-tuple-element.128), channel_id=1, source_target_pairs={{2,0},{4,2},{6,4},{8,6},{10,8},{12,10},{14,12},{16,14},{18,16},{20... | collective-permute-start | bytes 491528 | tf_op jit(solution)/shard_map/ppermute | solution.py:22
  52.1 9.7 %collective-permute-start.3 = (f32[40,1,1024]{2,0,1:T(8,128)S(1)}, f32[40,1,1024]{2,0,1:T(8,128)S(1)}, u32[]{:S(2)}, u32[]{:S(2)}) collective-permute-start(f32[40,1,1024]{2,0,1:T(8,128)S(1)} %get-tuple-element.129), channel_id=1, source_target_pairs={{0,2},{2,4},{4,6},{6,8},{8,10},{10,12},{12,14},{14,16},{16,18},{18... | collective-permute-start | bytes 491528 | tf_op jit(solution)/shard_map/ppermute | solution.py:19
  59.9 121.4 %copy-start.39 = (f32[9]{0:T(128)}, f32[9]{0:T(128)S(1)}, u32[]{:S(2)}) copy-start(f32[9]{0:T(128)S(1)} %scatter.16) | copy-start | bytes 112
  59.9 14.8 %copy-start.30 = (f32[9,9]{1,0:T(8,128)S(1)}, f32[9,9]{1,0:T(8,128)}, u32[]{:S(2)}) copy-start(f32[9,9]{1,0:T(8,128)} %constant.100.clone) | copy-start | bytes 976
  59.9 7.6 %copy-start.26 = (f32[40,1,1024]{2,0,1:T(8,128)}, f32[40,1,1024]{2,0,1:T(8,128)S(1)}, u32[]{:S(2)}) copy-start(f32[40,1,1024]{2,0,1:T(8,128)S(1)} %collective-permute-done.2) | copy-start | bytes 491524
  61.8 5.7 %copy-start.28 = (f32[40,1,1024]{2,0,1:T(8,128)}, f32[40,1,1024]{2,0,1:T(8,128)S(1)}, u32[]{:S(2)}) copy-start(f32[40,1,1024]{2,0,1:T(8,128)S(1)} %collective-permute-done.3) | copy-start | bytes 491524
  67.5 7.4 %copy-start.6 = (f32[40,16,1024]{2,0,1:T(8,128)}, f32[40,16,1024]{2,0,1:T(8,128)S(1)}, u32[]{:S(2)}) copy-start(f32[40,16,1024]{2,0,1:T(8,128)S(1)} %fusion.5) | copy-start | bytes 7864324
  68.3 9.0 %collective-permute-start.4 = (f32[40,1,1024]{2,0,1:T(8,128)}, f32[40,1,1024]{2,0,1:T(8,128)S(1)}, u32[]{:S(2)}, u32[]{:S(2)}) collective-permute-start(f32[40,1,1024]{2,0,1:T(8,128)} %get-tuple-element.126), channel_id=1, source_target_pairs={{2,0},{4,2},{6,4},{8,6},{10,8},{12,10},{14,12},{16,14},{18,16},{20... | collective-permute-start | bytes 491528 | tf_op jit(solution)/shard_map/ppermute | solution.py:22
  69.6 12.2 %collective-permute-start.5 = (f32[40,1,1024]{2,0,1:T(8,128)}, f32[40,1,1024]{2,0,1:T(8,128)S(1)}, u32[]{:S(2)}, u32[]{:S(2)}) collective-permute-start(f32[40,1,1024]{2,0,1:T(8,128)} %get-tuple-element.127), channel_id=1, source_target_pairs={{0,2},{2,4},{4,6},{6,8},{8,10},{10,12},{12,14},{14,16},{16,18},{18... | collective-permute-start | bytes 491528 | tf_op jit(solution)/shard_map/ppermute | solution.py:19
  74.9 108.1 %copy-start.24 = (f32[40,9]{0,1:T(8,128)}, f32[40,9]{0,1:T(8,128)S(1)}, u32[]{:S(2)}) copy-start(f32[40,9]{0,1:T(8,128)S(1)} %convolution_subtract_fusion.6) | copy-start | bytes 4324
  75.0 104.8 %copy-start.33 = (f32[40,9]{1,0:T(8,128)}, f32[40,9]{1,0:T(8,128)S(1)}, u32[]{:S(2)}) copy-start(f32[40,9]{1,0:T(8,128)S(1)} %copy.40) | copy-start | bytes 4324
  75.0 18.9 %copy-start.2 = (f32[40,16384]{1,0:T(8,128)S(1)}, f32[40,16384]{1,0:T(8,128)}, u32[]{:S(2)}) copy-start(f32[40,16384]{1,0:T(8,128)} %reduce-scatter.2.cloned.1.call-done) | copy-start | bytes 7864324
  81.8 121.4 %copy-start.21 = (f32[40,1,1024]{2,0,1:T(8,128)}, f32[40,1,1024]{2,0,1:T(8,128)S(1)}, u32[]{:S(2)}) copy-start(f32[40,1,1024]{2,0,1:T(8,128)S(1)} %collective-permute-done.5) | copy-start | bytes 491524
  87.3 11.2 %copy-start.19 = (f32[40,16,1024]{2,0,1:T(8,128)S(1)}, f32[40,16,1024]{2,0,1:T(8,128)}, u32[]{:S(2)}) copy-start(f32[40,16,1024]{2,0,1:T(8,128)} %copy-done.18) | copy-start | bytes 7864324
  87.3 11.2 %copy-start.27 = (f32[40,1,1024]{2,0,1:T(8,128)S(1)}, f32[40,1,1024]{2,0,1:T(8,128)}, u32[]{:S(2)}) copy-start(f32[40,1,1024]{2,0,1:T(8,128)} %copy-done.26) | copy-start | bytes 491524
  87.3 11.2 %copy-start.29 = (f32[40,1,1024]{2,0,1:T(8,128)S(1)}, f32[40,1,1024]{2,0,1:T(8,128)}, u32[]{:S(2)}) copy-start(f32[40,1,1024]{2,0,1:T(8,128)} %copy-done.28) | copy-start | bytes 491524
  87.4 8.9 %collective-permute-start.6 = (f32[40,1,1024]{2,0,1:T(8,128)S(1)}, f32[40,1,1024]{2,0,1:T(8,128)S(1)}, u32[]{:S(2)}, u32[]{:S(2)}) collective-permute-start(f32[40,1,1024]{2,0,1:T(8,128)S(1)} %get-tuple-element.124), channel_id=1, source_target_pairs={{2,0},{4,2},{6,4},{8,6},{10,8},{12,10},{14,12},{16,14},{18,16},{20... | collective-permute-start | bytes 491528 | tf_op jit(solution)/shard_map/ppermute | solution.py:22
  88.9 9.6 %collective-permute-start.7 = (f32[40,1,1024]{2,0,1:T(8,128)S(1)}, f32[40,1,1024]{2,0,1:T(8,128)S(1)}, u32[]{:S(2)}, u32[]{:S(2)}) collective-permute-start(f32[40,1,1024]{2,0,1:T(8,128)S(1)} %get-tuple-element.125), channel_id=1, source_target_pairs={{0,2},{2,4},{4,6},{6,8},{8,10},{10,12},{12,14},{14,16},{16,18},{18... | collective-permute-start | bytes 491528 | tf_op jit(solution)/shard_map/ppermute | solution.py:19
  183.8 19.5 %copy-start.4 = (f32[5,16,8,1024]{3,2,0,1:T(8,128)S(1)}, f32[5,16,8,1024]{3,2,0,1:T(8,128)}, u32[]{:S(2)}) copy-start(f32[5,16,8,1024]{3,2,0,1:T(8,128)} %copy-done.3) | copy-start | bytes 7864324
  183.8 19.5 %copy-start.7 = (f32[40,16,1024]{2,0,1:T(8,128)S(1)}, f32[40,16,1024]{2,0,1:T(8,128)}, u32[]{:S(2)}) copy-start(f32[40,16,1024]{2,0,1:T(8,128)} %copy-done.6) | copy-start | bytes 7864324
  183.8 19.5 %copy-start.17 = (f32[40,16,1024]{2,0,1:T(8,128)S(1)}, f32[40,16,1024]{2,0,1:T(8,128)}, u32[]{:S(2)}) copy-start(f32[40,16,1024]{2,0,1:T(8,128)} %get-tuple-element.109) | copy-start | bytes 7864324
  197.4 68.4 %copy-start.9 = (f32[40,16,1024]{2,0,1:T(8,128)}, f32[40,16,1024]{2,0,1:T(8,128)S(1)}, u32[]{:S(2)}) copy-start(f32[40,16,1024]{2,0,1:T(8,128)S(1)} %multiply_add_fusion.2) | copy-start | bytes 7864324
  197.4 11.7 %collective-permute-start.8 = (f32[40,1,1024]{2,0,1:T(8,128)S(1)}, f32[40,1,1024]{2,0,1:T(8,128)S(1)}, u32[]{:S(2)}, u32[]{:S(2)}) collective-permute-start(f32[40,1,1024]{2,0,1:T(8,128)S(1)} %get-tuple-element.118), channel_id=1, source_target_pairs={{2,0},{4,2},{6,4},{8,6},{10,8},{12,10},{14,12},{16,14},{18,16},{20... | collective-permute-start | bytes 491528 | tf_op jit(solution)/shard_map/ppermute | solution.py:22
  198.7 10.4 %collective-permute-start.9 = (f32[40,1,1024]{2,0,1:T(8,128)S(1)}, f32[40,1,1024]{2,0,1:T(8,128)S(1)}, u32[]{:S(2)}, u32[]{:S(2)}) collective-permute-start(f32[40,1,1024]{2,0,1:T(8,128)S(1)} %get-tuple-element.119), channel_id=1, source_target_pairs={{0,2},{2,4},{4,6},{6,8},{8,10},{10,12},{12,14},{14,16},{16,18},{18... | collective-permute-start | bytes 491528 | tf_op jit(solution)/shard_map/ppermute | solution.py:19
  203.3 5.8 %copy-start.36 = (f32[40]{0:T(128)S(1)}, f32[40]{0:T(128)}, u32[]{:S(2)}) copy-start(f32[40]{0:T(128)} %copy-done.35) | copy-start | bytes 484
  209.1 56.6 %copy-start.11 = (f32[40,16,1024]{2,0,1:T(8,128)}, f32[40,16,1024]{2,0,1:T(8,128)S(1)}, u32[]{:S(2)}) copy-start(f32[40,16,1024]{2,0,1:T(8,128)S(1)} %multiply_add_fusion.1) | copy-start | bytes 7864324
  210.6 55.1 %copy-start.13 = (f32[40,16,1024]{2,0,1:T(8,128)}, f32[40,16,1024]{2,0,1:T(8,128)S(1)}, u32[]{:S(2)}) copy-start(f32[40,16,1024]{2,0,1:T(8,128)S(1)} %fusion.14) | copy-start | bytes 7864324
  210.6 11.8 %collective-permute-start.10 = (f32[40,1,1024]{2,0,1:T(8,128)S(1)}, f32[40,1,1024]{2,0,1:T(8,128)S(1)}, u32[]{:S(2)}, u32[]{:S(2)}) collective-permute-start(f32[40,1,1024]{2,0,1:T(8,128)S(1)} %get-tuple-element.116), channel_id=1, source_target_pairs={{2,0},{4,2},{6,4},{8,6},{10,8},{12,10},{14,12},{16,14},{18,16},{20... | collective-permute-start | bytes 491528 | tf_op jit(solution)/shard_map/ppermute | solution.py:22
  211.9 10.5 %collective-permute-start.11 = (f32[40,1,1024]{2,0,1:T(8,128)S(1)}, f32[40,1,1024]{2,0,1:T(8,128)S(1)}, u32[]{:S(2)}, u32[]{:S(2)}) collective-permute-start(f32[40,1,1024]{2,0,1:T(8,128)S(1)} %get-tuple-element.117), channel_id=1, source_target_pairs={{0,2},{2,4},{4,6},{6,8},{8,10},{10,12},{12,14},{14,16},{16,18},{18... | collective-permute-start | bytes 491528 | tf_op jit(solution)/shard_map/ppermute | solution.py:19
  216.5 13.7 %collective-permute-start.16 = (f32[40,1,1024]{2,0,1:T(8,128)S(1)}, f32[40,1,1024]{2,0,1:T(8,128)S(1)}, u32[]{:S(2)}, u32[]{:S(2)}) collective-permute-start(f32[40,1,1024]{2,0,1:T(8,128)S(1)} %get-tuple-element.122), channel_id=1, source_target_pairs={{2,0},{4,2},{6,4},{8,6},{10,8},{12,10},{14,12},{16,14},{18,16},{20... | collective-permute-start | bytes 491528 | tf_op jit(solution)/shard_map/ppermute | solution.py:22
  217.8 12.4 %collective-permute-start.17 = (f32[40,1,1024]{2,0,1:T(8,128)S(1)}, f32[40,1,1024]{2,0,1:T(8,128)S(1)}, u32[]{:S(2)}, u32[]{:S(2)}) collective-permute-start(f32[40,1,1024]{2,0,1:T(8,128)S(1)} %get-tuple-element.123), channel_id=1, source_target_pairs={{0,2},{2,4},{4,6},{6,8},{8,10},{10,12},{12,14},{14,16},{16,18},{18... | collective-permute-start | bytes 491528 | tf_op jit(solution)/shard_map/ppermute | solution.py:19
  223.9 8.7 %collective-permute-start.12 = (f32[40,1,1024]{2,0,1:T(8,128)S(1)}, f32[40,1,1024]{2,0,1:T(8,128)S(1)}, u32[]{:S(2)}, u32[]{:S(2)}) collective-permute-start(f32[40,1,1024]{2,0,1:T(8,128)S(1)} %get-tuple-element.114), channel_id=1, source_target_pairs={{2,0},{4,2},{6,4},{8,6},{10,8},{12,10},{14,12},{16,14},{18,16},{20... | collective-permute-start | bytes 491528 | tf_op jit(solution)/shard_map/ppermute | solution.py:22
  225.2 9.3 %collective-permute-start.13 = (f32[40,1,1024]{2,0,1:T(8,128)S(1)}, f32[40,1,1024]{2,0,1:T(8,128)S(1)}, u32[]{:S(2)}, u32[]{:S(2)}) collective-permute-start(f32[40,1,1024]{2,0,1:T(8,128)S(1)} %get-tuple-element.115), channel_id=1, source_target_pairs={{0,2},{2,4},{4,6},{6,8},{8,10},{10,12},{12,14},{14,16},{16,18},{18... | collective-permute-start | bytes 491528 | tf_op jit(solution)/shard_map/ppermute | solution.py:19
  237.8 17.2 %copy-start.15 = (f32[40,16,1024]{2,0,1:T(8,128)}, f32[40,16,1024]{2,0,1:T(8,128)S(1)}, u32[]{:S(2)}) copy-start(f32[40,16,1024]{2,0,1:T(8,128)S(1)} %get-tuple-element.182) | copy-start | bytes 7864324
  237.9 17.2 %copy-start.16 = (f32[40,16,1024]{2,0,1:T(8,128)}, f32[40,16,1024]{2,0,1:T(8,128)S(1)}, u32[]{:S(2)}) copy-start(f32[40,16,1024]{2,0,1:T(8,128)S(1)} %get-tuple-element.181) | copy-start | bytes 7864324
  237.9 15.7 %collective-permute-start.18 = (f32[40,1,1024]{2,0,1:T(8,128)S(1)}, f32[40,1,1024]{2,0,1:T(8,128)S(1)}, u32[]{:S(2)}, u32[]{:S(2)}) collective-permute-start(f32[40,1,1024]{2,0,1:T(8,128)S(1)} %get-tuple-element.120), channel_id=1, source_target_pairs={{2,0},{4,2},{6,4},{8,6},{10,8},{12,10},{14,12},{16,14},{18,16},{20... | collective-permute-start | bytes 491528 | tf_op jit(solution)/shard_map/ppermute | solution.py:22
  239.2 14.4 %collective-permute-start.19 = (f32[40,1,1024]{2,0,1:T(8,128)S(1)}, f32[40,1,1024]{2,0,1:T(8,128)S(1)}, u32[]{:S(2)}, u32[]{:S(2)}) collective-permute-start(f32[40,1,1024]{2,0,1:T(8,128)S(1)} %get-tuple-element.121), channel_id=1, source_target_pairs={{0,2},{2,4},{4,6},{6,8},{8,10},{10,12},{12,14},{14,16},{16,18},{18... | collective-permute-start | bytes 491528 | tf_op jit(solution)/shard_map/ppermute | solution.py:19
  246.1 18.0 %collective-permute-start.14 = (f32[40,1,1024]{2,0,1:T(8,128)S(1)}, f32[40,1,1024]{2,0,1:T(8,128)}, u32[]{:S(2)}, u32[]{:S(2)}) collective-permute-start(f32[40,1,1024]{2,0,1:T(8,128)S(1)} %get-tuple-element.112), channel_id=1, source_target_pairs={{2,0},{4,2},{6,4},{8,6},{10,8},{12,10},{14,12},{16,14},{18,16},{20... | collective-permute-start | bytes 491528 | tf_op jit(solution)/shard_map/ppermute | solution.py:22
  247.4 16.7 %collective-permute-start.15 = (f32[40,1,1024]{2,0,1:T(8,128)S(1)}, f32[40,1,1024]{2,0,1:T(8,128)}, u32[]{:S(2)}, u32[]{:S(2)}) collective-permute-start(f32[40,1,1024]{2,0,1:T(8,128)S(1)} %get-tuple-element.113), channel_id=1, source_target_pairs={{0,2},{2,4},{4,6},{6,8},{8,10},{10,12},{12,14},{14,16},{16,18},{18... | collective-permute-start | bytes 491528 | tf_op jit(solution)/shard_map/ppermute | solution.py:19
  256.5 7.8 %collective-permute-start.20 = (f32[40,1,1024]{2,0,1:T(8,128)S(1)}, f32[40,1,1024]{2,0,1:T(8,128)}, u32[]{:S(2)}, u32[]{:S(2)}) collective-permute-start(f32[40,1,1024]{2,0,1:T(8,128)S(1)} %get-tuple-element.110), channel_id=1, source_target_pairs={{2,0},{4,2},{6,4},{8,6},{10,8},{12,10},{14,12},{16,14},{18,16},{20... | collective-permute-start | bytes 491528 | tf_op jit(solution)/shard_map/ppermute | solution.py:22
  257.8 7.9 %collective-permute-start.21 = (f32[40,1,1024]{2,0,1:T(8,128)S(1)}, f32[40,1,1024]{2,0,1:T(8,128)}, u32[]{:S(2)}, u32[]{:S(2)}) collective-permute-start(f32[40,1,1024]{2,0,1:T(8,128)S(1)} %get-tuple-element.111), channel_id=1, source_target_pairs={{0,2},{2,4},{4,6},{6,8},{8,10},{10,12},{12,14},{14,16},{16,18},{18... | collective-permute-start | bytes 491528 | tf_op jit(solution)/shard_map/ppermute | solution.py:19
  264.2 124.1 %copy-start.34 = (f32[40,9]{1,0:T(8,128)S(1)}, f32[40,9]{1,0:T(8,128)}, u32[]{:S(2)}) copy-start(f32[40,9]{1,0:T(8,128)} %copy-done.33) | copy-start | bytes 4324
  264.2 127.0 %copy-start.25 = (f32[40,9]{0,1:T(8,128)S(1)}, f32[40,9]{0,1:T(8,128)}, u32[]{:S(2)}) copy-start(f32[40,9]{0,1:T(8,128)} %copy-done.24) | copy-start | bytes 4324
  264.2 133.2 %copy-start.31 = (f32[9,9]{1,0:T(8,128)S(1)}, f32[9,9]{1,0:T(8,128)}, u32[]{:S(2)}) copy-start(f32[9,9]{1,0:T(8,128)} %constant.100.clone) | copy-start | bytes 976
  290.3 5.6 %copy-start.50 = (f32[40]{0:T(128)}, f32[40]{0:T(128)S(1)}, u32[]{:S(2)}) copy-start(f32[40]{0:T(128)S(1)} %get-tuple-element.75) | copy-start | bytes 484
  290.3 5.6 %copy-start.51 = (f32[40]{0:T(128)}, f32[40]{0:T(128)S(1)}, u32[]{:S(2)}) copy-start(f32[40]{0:T(128)S(1)} %get-tuple-element.76) | copy-start | bytes 484
  290.3 7.0 %copy-start.45 = (f32[40]{0:T(128)}, f32[40]{0:T(128)S(1)}, u32[]{:S(2)}) copy-start(f32[40]{0:T(128)S(1)} %get-tuple-element.83) | copy-start | bytes 484
  290.3 7.0 %copy-start.46 = (f32[40]{0:T(128)}, f32[40]{0:T(128)S(1)}, u32[]{:S(2)}) copy-start(f32[40]{0:T(128)S(1)} %get-tuple-element.84) | copy-start | bytes 484
  290.3 8.4 %copy-start.44 = (f32[40]{0:T(128)}, f32[40]{0:T(128)S(1)}, u32[]{:S(2)}) copy-start(f32[40]{0:T(128)S(1)} %get-tuple-element.82) | copy-start | bytes 484
  290.3 8.4 %copy-start.47 = (f32[40]{0:T(128)}, f32[40]{0:T(128)S(1)}, u32[]{:S(2)}) copy-start(f32[40]{0:T(128)S(1)} %get-tuple-element.85) | copy-start | bytes 484
  290.4 9.7 %copy-start.48 = (f32[40]{0:T(128)}, f32[40]{0:T(128)S(1)}, u32[]{:S(2)}) copy-start(f32[40]{0:T(128)S(1)} %get-tuple-element.86) | copy-start | bytes 484
  290.4 9.7 %copy-start.49 = (f32[40]{0:T(128)}, f32[40]{0:T(128)S(1)}, u32[]{:S(2)}) copy-start(f32[40]{0:T(128)S(1)} %get-tuple-element.87) | copy-start | bytes 484
  290.4 11.0 %copy-start.42 = (f32[40]{0:T(128)}, f32[40]{0:T(128)S(1)}, u32[]{:S(2)}) copy-start(f32[40]{0:T(128)S(1)} %get-tuple-element.80) | copy-start | bytes 484
  290.4 11.0 %copy-start.43 = (f32[40]{0:T(128)}, f32[40]{0:T(128)S(1)}, u32[]{:S(2)}) copy-start(f32[40]{0:T(128)S(1)} %get-tuple-element.81) | copy-start | bytes 484
  422.1 24.2 %copy-start.10 = (f32[40,16,1024]{2,0,1:T(8,128)S(1)}, f32[40,16,1024]{2,0,1:T(8,128)}, u32[]{:S(2)}) copy-start(f32[40,16,1024]{2,0,1:T(8,128)} %copy-done.9) | copy-start | bytes 7864324
  422.2 24.2 %copy-start.12 = (f32[40,16,1024]{2,0,1:T(8,128)S(1)}, f32[40,16,1024]{2,0,1:T(8,128)}, u32[]{:S(2)}) copy-start(f32[40,16,1024]{2,0,1:T(8,128)} %copy-done.11) | copy-start | bytes 7864324
  422.2 24.2 %copy-start.14 = (f32[40,16,1024]{2,0,1:T(8,128)S(1)}, f32[40,16,1024]{2,0,1:T(8,128)}, u32[]{:S(2)}) copy-start(f32[40,16,1024]{2,0,1:T(8,128)} %copy-done.13) | copy-start | bytes 7864324
  446.5 15.8 %copy-start.1 = (bf16[80,136]{0,1:T(8,128)(2,1)S(1)}, bf16[80,136]{0,1:T(8,128)(2,1)}, u32[]{:S(2)}) copy-start(bf16[80,136]{0,1:T(8,128)(2,1)} %param.13) | copy-start | bytes 65284
  (32 other events, 96.6 us)
Sparse Core Ops, SparseCore 0:
  17.1 15.7 reduce-scatter.1
where the time goes:
time: 471 us; the launch traced here: 469 us
  blocking collectives  153 us (32%)
  other arithmetic  124 us (26%)
  starting transfers between devices  71.4 us (15%)
  local copies, waits for them, and re-layouts  55.5 us (12%)
  waiting for transfers between devices  41.9 us (9%)
  between operations  16.7 us (4%)
  matrix products  7.1 us (2%)
    psum x2, blocking collectives, shards(): gram = lax.psum(gram, 'tile')  153 us
    ppermute x11, starting transfers between devices, extended(): lax.ppermute(lax.slice_in_dim(block, block.shape[dim] - width, None, axis...  56.9 us
    add x3, other arithmetic, combine(): total = total + coef[:, index, None, None] * vectors[index]  38.5 us
    reduce_sum x3, other arithmetic, inner_table(): jnp.sum(vectors[first] * vectors[second], axis=(1, 2))  30.2 us
    unnamed x180, local copies, waits for them, and re-layouts  29.2 us
    mul x7, other arithmetic, stencil_rows(): return weight_col * beside_all  20.1 us
    ppermute x11, waiting for transfers between devices, extended(): lax.ppermute(lax.slice_in_dim(block, block.shape[dim] - width, None, axis...  16.6 us
    reduce_scatter x1, waiting for transfers between devices, shards(): lax.psum_scatter(jnp.dot(own_cols, flat, preferred_element_type=jnp.float...  15.9 us
  transfers between devices with their start and end apart: 23, of which 12 were waited for; matrix products, arithmetic and copies ran while one was open for 2% of the time, Pallas kernels for 0%

commit v1 on v0

v1 whole, which is shorter than its diff:
```python
import functools

import jax
import jax.numpy as jnp
from jax import lax
from jax.experimental import pallas as pl
from jax.experimental.pallas import tpu as pltpu
from jax.sharding import PartitionSpec as P

S = 4
HALO = 2 * S
POWER = 13
UNROLL = 1
SUB = 8
LANE = 128
MESH = pl.DeviceIdType.MESH
f32 = jnp.float32
bf16 = jnp.bfloat16


def stage_groups(count):
    groups = []
    while count > 1:
        size = 4 if count % 4 == 0 else (2 if count % 2 == 0 else count)
        groups.append(size)
        count //= size
    return groups


def encode(value, scale):
    a = value * scale
    a4 = (a * a) * (a * a)
    return ((a4 * a4) * (a4 * a)).astype(bf16)


def decode(code, scale):
    code = code.astype(f32)
    size = jnp.exp(jnp.log(jnp.maximum(jnp.abs(code), 2.0 ** -126)) * (1.0 / POWER)) * (1.0 / scale)
    return jnp.where(code > 0.0, size, jnp.where(code < 0.0, -size, 0.0))


def spread(tile, times):
    return jnp.concatenate([tile] * times, axis=1)


def add(left, right):
    if left is None:
        return right
    if right is None:
        return left
    return left + right


def scaled(factor, vector):
    return [None if entry is None else factor * entry for entry in vector]


def added(left, right):
    return [add(a, b) for a, b in zip(left, right)]


def minus(left, right):
    result = []
    for a, b in zip(left, right):
        if b is None:
            result.append(a)
        elif a is None:
            result.append(-b)
        else:
            result.append(a - b)
    return result


def form(gram, left, right):
    total = None
    for a, left_entry in enumerate(left):
        if left_entry is None:
            continue
        inner = None
        for b, right_entry in enumerate(right):
            if right_entry is not None:
                inner = add(inner, gram(a, b) * right_entry)
        total = add(total, left_entry * inner)
    return total


def recurrence(gram, shift, p_coef, r_coef):
    x_coef = [None] * len(p_coef)
    squares = form(gram, r_coef, r_coef)
    for step in range(S):
        moved = minus(p_coef, shift(p_coef))
        alpha = squares / form(gram, p_coef, moved)
        x_coef = added(x_coef, scaled(alpha, p_coef))
        r_coef = minus(r_coef, scaled(alpha, moved))
        fresh = form(gram, r_coef, r_coef)
        p_coef = added(r_coef, scaled(fresh / squares, p_coef))
        squares = fresh
    return x_coef, r_coef, p_coef


def kernel(tiles, levs, groups, rows, modes, cells, levels, inc_ref, proj_ref, helm_ref, sol_ref, res_ref,
           x_all, wide, fields, dirs, res0, extra, total, out_buf, in_buf, weights, sums, coefs, grams,
           local_sems, swap_send, swap_recv, halo_send, halo_recv, gram_send, gram_recv):
    tile = lax.axis_index("tile")
    lev = lax.axis_index("lev")
    part = inc_ref.shape[0]
    across = cells // LANE
    parts_m = modes // SUB
    barrier = pltpu.get_barrier_semaphore()

    stage_peers = []
    stride = 1
    for size in groups:
        digit = lax.rem(lax.div(tile, stride), size)
        base = tile - digit * stride
        peers = []
        for j in range(1, size):
            peers.append(base + lax.rem(digit + j, size) * stride)
        stage_peers.append((digit, peers))
        stride *= size

    count = 0
    for j in range(1, levs):
        pl.semaphore_signal(barrier, 1, device_id=(tile, lax.rem(lev + j, levs)), device_id_type=MESH)
        count += 1
    for peer in (lax.rem(tile + 1, tiles), lax.rem(tile + tiles - 1, tiles)):
        pl.semaphore_signal(barrier, 1, device_id=(peer, lev), device_id_type=MESH)
        count += 1
    for digit, peers in stage_peers:
        for peer in peers:
            pl.semaphore_signal(barrier, 1, device_id=(peer, lev), device_id_type=MESH)
            count += 1

    local = pltpu.make_async_copy(inc_ref, x_all.at[0], local_sems.at[0])
    local.start()

    proj = proj_ref[...].astype(f32)
    own = proj[0:modes]
    for j in range(1, levs):
        own = jnp.where(lev == j, proj[j * modes:(j + 1) * modes], own)
    own_levels = levels // levs
    groups_l = [own[:, j * own_levels:(j + 1) * own_levels] for j in range(levs)]
    depth = part
    col_e = lax.broadcasted_iota(jnp.int32, (own_levels, depth), 1)
    row_e = lax.broadcasted_iota(jnp.int32, (own_levels, depth), 0) * rows
    onehot = jnp.where((col_e >= row_e) & (col_e < row_e + rows), 1.0, 0.0).astype(bf16)
    col_w = lax.rem(lax.broadcasted_iota(jnp.int32, (2 * modes, depth), 1), rows)
    second = jnp.where(lax.broadcasted_iota(jnp.int32, (2 * modes, depth), 0) >= modes, 1, 0)
    pick = col_w - second

    def widen(position):
        chosen = groups_l[position]
        for j in range(1, levs):
            chosen = jnp.where(lev == j, groups_l[(j + position) % levs], chosen)
        twice = jnp.concatenate([chosen, chosen], axis=0).astype(bf16)
        repeated = jnp.dot(twice, onehot, preferred_element_type=f32)
        for pair in range(rows // 2):
            wide[position, pair * 2 * modes:(pair + 1) * 2 * modes, :] = jnp.where(
                pick == 2 * pair, repeated, 0.0).astype(bf16)

    widen(0)
    pl.semaphore_wait(barrier, count)
    swaps = []
    for j in range(1, levs):
        copy = pltpu.make_async_remote_copy(
            src_ref=inc_ref, dst_ref=x_all.at[levs - j], send_sem=swap_send.at[j - 1],
            recv_sem=swap_recv.at[j - 1], device_id=(tile, lax.rem(lev + j, levs)), device_id_type=MESH)
        copy.start()
        swaps.append(copy)

    diag = lax.broadcasted_iota(jnp.int32, (modes, modes), 0) == lax.broadcasted_iota(jnp.int32, (modes, modes), 1)
    helm = jnp.sum(jnp.where(diag, jnp.broadcast_to(helm_ref[...], (modes, modes)), 0.0), axis=1, keepdims=True)
    weight = jnp.broadcast_to(1.0 / (4.0 + helm), (modes, LANE))
    weights[0] = weight
    weights[1] = jnp.where(tile > 0, weight, 0.0)
    weights[2] = jnp.where(tile < tiles - 1, weight, 0.0)
    sums[...] = jnp.zeros_like(sums)

    base_row = HALO
    field = fields.at[0]
    block = 2 * LANE if cells % (2 * LANE) == 0 else LANE

    def project_part(position):
        def project(index, carry):
            cols = pl.ds(pl.multiple_of(index * block, block), block)
            got = jnp.dot(wide[position], x_all[position, :, cols], preferred_element_type=f32)
            got = got.reshape(rows, modes, block)
            if position:
                got = field[base_row:base_row + rows, :, cols] + got
            field[base_row:base_row + rows, :, cols] = got
            return carry

        lax.fori_loop(0, cells // block, project, 0)

    local.wait()
    project_part(0)
    for j in range(1, levs):
        widen(j)
    for j in range(1, levs):
        swaps[j - 1].wait()
    for j in range(1, levs):
        project_part(j)

    slots = HALO // 2
    scale = 2.0 ** 9.7 / (0.5 * 30.0 * levels)

    def own_pair(side, pair):
        first = 2 * pair if side == 0 else rows - 2 - 2 * pair
        return field[base_row + first:base_row + first + 2].reshape(2 * modes, cells)

    def halo_copy(side, slot):
        peer = lax.rem(tile + tiles - 1, tiles) if side == 0 else lax.rem(tile + 1, tiles)
        return pltpu.make_async_remote_copy(
            src_ref=out_buf.at[side, slot], dst_ref=in_buf.at[side, slot], send_sem=halo_send.at[side, slot],
            recv_sem=halo_recv.at[side, slot], device_id=(peer, lev), device_id_type=MESH)

    for slot in range(slots):
        for side in range(2):
            out_buf[side, slot] = encode(own_pair(side, slot), scale)

        @pl.when(tile > 0)
        def _(slot=slot):
            halo_copy(0, slot).start()

        @pl.when(tile < tiles - 1)
        def _(slot=slot):
            halo_copy(1, slot).start()

    has = {0: tile < tiles - 1, 1: tile > 0}

    def take(side, pair):
        first = base_row + rows + 2 * pair if side == 0 else base_row - 2 - 2 * pair

        @pl.when(has[side])
        def _():
            halo_copy(side, pair).wait_recv()
            field[first:first + 2] = decode(in_buf[side, pair], scale).reshape(2, modes, cells)

        @pl.when(jnp.logical_not(has[side]))
        def _():
            field[first:first + 2] = jnp.zeros((2, modes, cells), f32)

    lane = lax.broadcasted_iota(jnp.int32, (SUB, LANE), 1)
    first_lane = lane == 0
    last_lane = lane == LANE - 1
    nothing = jnp.zeros((SUB, LANE), f32)

    def beside(tile_row):
        pieces = [tile_row[:, j * LANE:(j + 1) * LANE] for j in range(across)]
        right = [pltpu.roll(piece, 1, 1) for piece in pieces]
        left = [pltpu.roll(piece, LANE - 1, 1) for piece in pieces]
        result = []
        for j in range(across):
            low = jnp.where(first_lane, right[j - 1] if j else nothing, right[j])
            high = jnp.where(last_lane, left[j + 1] if j + 1 < across else nothing, left[j])
            result.append(low + high)
        return jnp.concatenate(result, axis=1)

    def fold(product):
        pieces = [product[:, j * LANE:(j + 1) * LANE] for j in range(across)]
        while len(pieces) > 1:
            pieces = [pieces[i] + pieces[i + 1] if i + 1 < len(pieces) else pieces[i] for i in range(0, len(pieces), 2)]
        return pieces[0]

    def over_rows(low, high, body):
        if high <= low:
            return
        if high - low == 1:
            body(low)
            return

        def step(index, carry):
            body(index)
            return carry

        lax.fori_loop(low, high, step, 0, unroll=UNROLL if (high - low) % UNROLL == 0 else 1)

    def apply(src, src_off, dst, dst_off, low, high, pairs=(), which=0):
        def body(row):
            for m in range(parts_m):
                at = slice(m * SUB, (m + 1) * SUB)
                here = src[row + src_off, at, :]
                around = src[row + src_off - 1, at, :] + src[row + src_off + 1, at, :] + beside(here)
                fresh = spread(weights[which, at, :], across) * around
                dst[row + dst_off, at, :] = fresh
                cache = {"src": here, "dst": fresh}
                for slot, left, right in pairs:
                    values = []
                    for operand in (left, right):
                        if isinstance(operand, str):
                            values.append(cache[operand])
                        else:
                            ref, off = operand
                            values.append(ref[row + off, at, :])
                    sums[slot, at, :] = sums[slot, at, :] + fold(values[0] * values[1])

        over_rows(low, high, body)

    def apply_all(src, src_off, dst, dst_off, wide_by, pairs):
        apply(src, src_off, dst, dst_off, -wide_by, 0, which=1)
        apply(src, src_off, dst, dst_off, 0, rows, pairs)
        apply(src, src_off, dst, dst_off, rows, rows + wide_by, which=2)

    def power_pairs(power):
        found = [(2 * power - 1, "src", "dst"), (2 * power, "dst", "dst")]
        if power == 1:
            found.append((0, "src", "src"))
        return found

    for power in range(1, S + 1):
        apply(fields.at[power - 1], HALO, fields.at[power], HALO, power, rows - power, power_pairs(power))
    for pair in range(S // 2):
        for side in range(2):
            take(side, pair)
    for power in range(1, S + 1):
        src, dst = fields.at[power - 1], fields.at[power]
        found = power_pairs(power)
        apply(src, HALO, dst, HALO, power - S, 0, which=1)
        apply(src, HALO, dst, HALO, 0, power, found)
        apply(src, HALO, dst, HALO, rows - power, rows, found)
        apply(src, HALO, dst, HALO, rows, rows + S - power, which=2)

    def packed(number):
        lanes = lax.broadcasted_iota(jnp.int32, (modes, LANE), 1)
        table = jnp.zeros((modes, LANE), f32)
        for slot in range(number):
            table = jnp.where(lanes == slot, jnp.sum(sums[slot], axis=1, keepdims=True), table)
        return table

    def gram_copies(block_index, stage):
        digit, peers = stage_peers[stage]
        size = groups[stage]
        sends = []
        for j in range(1, size):
            sends.append(pltpu.make_async_remote_copy(
                src_ref=grams.at[block_index, stage, digit], dst_ref=grams.at[block_index, stage, digit],
                send_sem=gram_send.at[block_index, stage, j - 1], recv_sem=gram_recv.at[block_index, stage, digit],
                device_id=(peers[j - 1], lev), device_id_type=MESH))
        return sends

    def gram_start(block_index, stage, table):
        grams[block_index, stage, stage_peers[stage][0]] = table
        for copy in gram_copies(block_index, stage):
            copy.start()

    def gram_finish(block_index, stage):
        digit, peers = stage_peers[stage]
        size = groups[stage]
        for copy in gram_copies(block_index, stage):
            copy.wait_send()
        for j in range(1, size):
            sender = lax.rem(digit + j, size)
            pltpu.make_async_remote_copy(
                src_ref=grams.at[block_index, stage, sender], dst_ref=grams.at[block_index, stage, sender],
                send_sem=gram_send.at[block_index, stage, j - 1], recv_sem=gram_recv.at[block_index, stage, sender],
                device_id=(peers[j - 1], lev), device_id_type=MESH).wait_recv()
        table = grams[block_index, stage, 0]
        for j in range(1, size):
            table = table + grams[block_index, stage, j]
        return table

    def column(table, slot):
        return jnp.broadcast_to(table[:, slot:slot + 1], (modes, LANE))

    def finish_all(block_index, table):
        for stage in range(len(groups)):
            if stage:
                gram_start(block_index, stage, table)
            table = gram_finish(block_index, stage)
        return table

    table = packed(2 * S + 1)
    gram_start(0, 0, table)

    for pair in range(S // 2, HALO // 2):
        for side in range(2):
            take(side, pair)
    for power in range(1, S + 1):
        src, dst = fields.at[power - 1], fields.at[power]
        apply(src, HALO, dst, HALO, power - HALO, power - S, which=1)
        apply(src, HALO, dst, HALO, rows + S - power, rows + HALO - power, which=2)
    sums[...] = jnp.zeros_like(sums)

    table = finish_all(0, table)
    moments = [column(table, slot) for slot in range(2 * S + 1)]
    one = jnp.ones((modes, LANE), f32)
    start = [one] + [None] * S
    x_coef, r_coef, p_coef = recurrence(
        lambda a, b: moments[a + b], lambda vector: [None] + vector[:-1], start, start)

    def keep(lists):
        position, kept = 0, []
        for entries in lists:
            places = []
            for index, entry in enumerate(entries):
                if entry is not None:
                    coefs[position] = entry
                    places.append((index, position))
                    position += 1
            kept.append(places)
        return kept

    def combined(places, values, at):
        result = None
        for index, position in places:
            result = add(result, spread(coefs[position, at, :], across) * values[index])
        return result

    x_at, r_at, p_at = keep([x_coef, r_coef, p_coef])

    def mix(low, high, inside):
        def body(row):
            for m in range(parts_m):
                at = slice(m * SUB, (m + 1) * SUB)
                values = [fields[power, row + HALO, at, :] for power in range(S + 1)]
                if inside:
                    total[row, at, :] = combined(x_at, values, at)
                res0[row + S, at, :] = combined(r_at, values, at)
                dirs[row + S, at, :] = combined(p_at, values, at)

        over_rows(low, high, body)

    mix(-S, 0, False)
    mix(0, rows, True)
    mix(rows, rows + S, False)

    d_refs = [(dirs, S)] + [(fields.at[power], HALO) for power in range(1, S + 1)]
    r_refs = [(res0, S), (fields.at[0], HALO)] + [(extra.at[power], S) for power in range(S - 2)]
    md, mr, cross = 0, 2 * S + 1, 4 * S
    for power in range(1, S + 1):
        found = [(md + 2 * power - 1, "src", "dst"), (md + 2 * power, "dst", "dst")]
        if power == 1:
            found.append((md, "src", "src"))
        apply_all(*d_refs[power - 1], *d_refs[power], S - power, found)
    for power in range(1, S):
        found = [(mr + 2 * power - 1, "src", "dst"), (mr + 2 * power, "dst", "dst"),
                 (cross + 2 * power, d_refs[power], "dst"), (cross + 2 * power + 1, d_refs[power + 1], "dst")]
        if power == 1:
            found += [(mr, "src", "src"), (cross, d_refs[0], "src"), (cross + 1, d_refs[1], "src")]
        apply_all(*r_refs[power - 1], *r_refs[power], S - 1 - power, found)

    number = 6 * S
    table = packed(number)
    gram_start(1, 0, table)
    table = finish_all(1, table)
    moments = [column(table, slot) for slot in range(number)]

    def gram(a, b):
        if a > S and b > S:
            return moments[mr + a + b - 2 * S - 2]
        if a > S or b > S:
            return moments[cross + a + b - S - 1]
        return moments[md + a + b]

    def shift(vector):
        return [None] + vector[:S] + [None] + vector[S + 1:2 * S]

    x_coef, r_coef, p_coef = recurrence(
        gram, shift, [one] + [None] * (2 * S), [None] * (S + 1) + [one] + [None] * (S - 1))
    x_at, r_at = keep([x_coef, r_coef])

    def last(row):
        for m in range(parts_m):
            at = slice(m * SUB, (m + 1) * SUB)
            values = [ref[row + off, at, :] for ref, off in d_refs + r_refs]
            total[row, at, :] = total[row, at, :] + combined(x_at, values, at)
            dirs[row + S, at, :] = combined(r_at, values, at)

    chunk = rows // 2
    writes = []
    for index in range(2):
        over_rows(index * chunk, (index + 1) * chunk, last)
        rng = pl.ds(index * chunk, chunk)
        copy = pltpu.make_async_copy(total.at[rng], sol_ref.at[rng], local_sems.at[1 + 2 * index])
        copy.start()
        writes.append(copy)
        copy = pltpu.make_async_copy(dirs.at[pl.ds(S + index * chunk, chunk)], res_ref.at[rng], local_sems.at[2 + 2 * index])
        copy.start()
        writes.append(copy)

    for slot in range(slots):
        @pl.when(tile > 0)
        def _(slot=slot):
            halo_copy(0, slot).wait_send()

        @pl.when(tile < tiles - 1)
        def _(slot=slot):
            halo_copy(1, slot).wait_send()
    for copy in writes:
        copy.wait()


def shards(increments, projection, helmholtz):
    tiles, levs = lax.axis_size("tile"), lax.axis_size("lev")
    own_levels, rows, cells = increments.shape
    modes = projection.shape[0] // levs
    levels = own_levels * levs
    groups = stage_groups(tiles)
    most = max(groups)
    slots = HALO // 2
    vmem = pltpu.VMEM
    dma = pltpu.SemaphoreType.DMA
    scratch = [
        vmem((levs, own_levels * rows, cells), bf16),
        vmem((levs, rows * modes, own_levels * rows), bf16),
        vmem((S + 1, rows + 2 * HALO, modes, cells), f32),
        vmem((rows + 2 * S, modes, cells), f32),
        vmem((rows + 2 * S, modes, cells), f32),
        vmem((S - 2, rows + 2 * S, modes, cells), f32),
        vmem((rows, modes, cells), f32),
        vmem((2, slots, 2 * modes, cells), bf16),
        vmem((2, slots, 2 * modes, cells), bf16),
        vmem((3, modes, LANE), f32),
        vmem((6 * S, modes, LANE), f32),
        vmem((6 * S, modes, LANE), f32),
        vmem((2, len(groups), most, modes, LANE), f32),
        dma((5,)),
        dma((levs - 1,)),
        dma((levs - 1,)),
        dma((2, slots)),
        dma((2, slots)),
        dma((2, len(groups), most)),
        dma((2, len(groups), most)),
    ]
    shape = jax.ShapeDtypeStruct((rows, modes, cells), f32)
    solved, resid = pl.pallas_call(
        functools.partial(kernel, tiles, levs, groups, rows, modes, cells, levels),
        out_shape=(shape, shape),
        in_specs=[pl.BlockSpec(memory_space=pl.ANY), pl.BlockSpec(memory_space=pltpu.VMEM),
                  pl.BlockSpec(memory_space=pltpu.VMEM)],
        out_specs=(pl.BlockSpec(memory_space=pl.ANY), pl.BlockSpec(memory_space=pl.ANY)),
        scratch_shapes=scratch,
        compiler_params=pltpu.CompilerParams(collective_id=0, has_side_effects=True, vmem_limit_bytes=67000000),
    )(increments.reshape(own_levels * rows, cells), projection, helmholtz.reshape(1, modes))
    return jnp.transpose(solved, (1, 0, 2)), jnp.transpose(resid, (1, 0, 2))


def solution(mesh):
    in_specs = (P("lev", "tile", None), P(), P("lev"))
    out_specs = (P("lev", "tile", None), P("lev", "tile", None))
    return jax.shard_map(shards, mesh=mesh, in_specs=in_specs, out_specs=out_specs, check_vma=False)
```

time: 471 us -> 101 us (0.21)
  blocking collectives: 153 us -> 0 us
  other arithmetic: 124 us -> 0 us
  Pallas kernels: 0 us -> 90.2 us
  starting transfers between devices: 71.4 us -> 0 us
  local copies, waits for them, and re-layouts: 55.5 us -> 9.39 us
  waiting for transfers between devices: 41.9 us -> 0 us
  between operations: 16.7 us -> 0.65 us
  matrix products: 7.1 us -> 0 us
    psum x2 -> x0, blocking collectives: 153 us -> none  [shards(): gram = lax.psum(gram, 'tile')]
    pallas_call x0 -> x1, Pallas kernels: none -> 90.2 us  [shards(): pl.pallas_call(functools.partial(kernel, tiles, levs, groups, rows, modes...]
    ppermute x22 -> x0, starting transfers between devices: 71.4 us -> none  [the longest x11 56.9 us: extended(): lax.ppermute(lax.slice_in_dim(block, block.shape[dim] - width, None, axis...]
    add x11 -> x0, other arithmetic: 54.5 us -> none  [the longest x3 38.5 us: combine(): total = total + coef[:, index, None, None] * vectors[index]]
    reduce_sum x3 -> x0, other arithmetic: 30.2 us -> none  [inner_table(): jnp.sum(vectors[first] * vectors[second], axis=(1, 2))]
    ppermute x22 -> x0, waiting for transfers between devices: 25.9 us -> none  [the longest x11 16.6 us: extended(): lax.ppermute(lax.slice_in_dim(block, block.shape[dim] - width, None, axis...]
    mul x7 -> x0, other arithmetic: 20.1 us -> none  [stencil_rows(): return weight_col * beside_all]
    unnamed x180 -> x5, local copies, waits for them, and re-layouts: 29.2 us -> 9.39 us
  transfers between devices with their start and end apart: 23 -> 0, of which waited for: 12 -> 0; matrix products, arithmetic and copies ran while one was open for 2% -> 0% of each run, Pallas kernels for 0% -> 0%
where the time goes in v1:
time: 101 us; the launch traced here: 100 us
  Pallas kernels  90.2 us (89%)
  local copies, waits for them, and re-layouts  9.39 us (9%)
    pallas_call x1, Pallas kernels, shards(): pl.pallas_call(functools.partial(kernel, tiles, levs, groups, rows, modes...  90.2 us
    unnamed x5, local copies, waits for them, and re-layouts  9.39 us

profile of v1, /device:TPU:0, one launch (start us, length us, event | category | flops | bytes accessed | tf_op | source)
XLA Modules:
  0.0 100.3 jit_solution(4801404587069478540)
XLA Ops:
  0.6 1.5 %copy.5.proj_ref = bf16[80,136]{1,0:T(8,128)(2,1)} copy(bf16[80,136]{0,1:T(8,128)(2,1)} %param.4) | data formatting | bytes 43520 | tf_op args[1]
  2.1 90.2 %shard_map.50 = (f32[16,40,1024]{2,1,0:T(8,128)}, f32[16,40,1024]{2,1,0:T(8,128)}) custom-call(bf16[1088,1024]{1,0:T(8,128)(2,1)} %bitcast.6, bf16[80,136]{1,0:T(8,128)(2,1)} %copy.5.proj_ref, f32[1,40]{1,0:T(1,128)} %bitcast.7), custom_call_target="tpu_custom_call" | custom-call | tf_op jit(solution)/shard_map/pallas_call | solution.py:526
  92.3 0.0 copy-start
  92.3 4.9 %copy.6 = f32[40,16,1024]{2,1,0:T(8,128)} copy(f32[40,16,1024]{2,0,1:T(8,128)} %bitcast.5) | data formatting | bytes 5242880
  97.2 0.0 copy-done
  97.2 3.0 %copy.7 = f32[40,16,1024]{2,1,0:T(8,128)} copy(f32[40,16,1024]{2,0,1:T(8,128)S(1)} %bitcast.4) | data formatting | bytes 5242880
Async XLA Ops:
  92.3 4.9 %copy-start = (f32[16,40,1024]{2,1,0:T(8,128)S(1)}, f32[16,40,1024]{2,1,0:T(8,128)}, u32[]{:S(2)}) copy-start(f32[16,40,1024]{2,1,0:T(8,128)} %get-tuple-element.5) | copy-start | bytes 7864324
